TPU v7x, 32 devices: a whole 2x2x4 slice. The times are simulated.
32 devices in a mesh: seq: 8 (over z, y), tensor: 4 (over x, core).
Axes of the slice: x: 2, y: 2, z: 4, core: 2. Of those that a mesh axis runs over, the one named last changes fastest.
Arguments:
- layer_input: bfloat16 [2048, 4096], P('seq', 'tensor'), may hold values from -6 to 6
- norm_gain: float32 [4096], replicated, may hold values from 0.1 to 1.9
- in_weights: bfloat16 [2, 4096, 2048], P(None, None, 'tensor'), may hold values from -0.09375 to 0.09375
- conv_weight: float32 [4, 2048], P(None, 'tensor'), may hold values from -4 to 4
- conv_bias: float32 [2048], P('tensor'), may hold values from -3 to 3
- gate_weights: bfloat16 [2, 8, 256, 256], P(None, 'tensor'), may hold values from -0.375 to 0.375
- gate_bias: float32 [2, 2048], P(None, 'tensor'), may hold values from -4 to 4
- decay_rate: float32 [2048], P('tensor'), may hold values from 1e-06 to 0.03, as said below
- out_weight: bfloat16 [2048, 4096], P('tensor'), may hold values from -0.1875 to 0.1875
- mlp_gain: float32 [4096], replicated, may hold values from 0.1 to 1.9
- mlp_in: bfloat16 [2, 4096, 6144], P(None, 'seq', 'tensor'), may hold values from -0.09375 to 0.09375
- mlp_out: bfloat16 [6144, 4096], P('tensor', 'seq'), may hold values from -0.109375 to 0.109375
Outputs:
- block_output: bfloat16 [2048, 4096], P('seq', 'tensor')
Inputs may be any that keep to these rules, and one draw needn't show every extreme that they name: `decay_rate`: every rate is positive.
All inputs are finite; a program needn't handle non-finite values.
Results may differ from a plain program's by a relative error of at most 0.015.
Values may be sent and summed in bfloat16 or wider, within the bound.
A program may use at most 128 MiB of HBM per device.

v0:
```python
import jax
import jax.numpy as jnp
from jax import lax
from jax.sharding import PartitionSpec as P


def shifted(value, axis, steps):
    count = lax.axis_size(axis)
    first, last = (max(0, -steps), min(count, count - steps))
    return lax.ppermute(value, axis, [(source, source + steps) for source in range(first, last)])


def prefix(value, axis, combine, identity):
    size, here = (lax.axis_size(axis), lax.axis_index(axis))
    everything = jax.tree.map(lambda part: lax.all_gather(part, axis), value)
    start = jax.tree.map(
        lambda part, zero: jnp.broadcast_to(jnp.asarray(zero, part.dtype), part.shape),
        value,
        identity,
    )

    def hop(k, before):
        reached = k < here
        new = combine(before, jax.tree.map(lambda part: part[k], everything))
        return jax.tree.map(lambda a, b: jnp.where(reached, a, b), new, before)

    return lax.fori_loop(0, size, hop, start)


def rms_scale(rows, gain):
    values = rows.astype(jnp.float32)
    mean_square = jnp.mean(values * values, axis=-1, keepdims=True)
    return (values * lax.rsqrt(mean_square + 1e-06) * gain).astype(jnp.bfloat16)


def chain_step(earlier, later):
    return (earlier[0] * later[0], later[0] * earlier[1] + later[1])


def shards(
    layer_input,
    norm_gain,
    in_weights,
    conv_weight,
    conv_bias,
    gate_weights,
    gate_bias,
    decay_rate,
    out_weight,
    mlp_gain,
    mlp_in,
    mlp_out,
):
    whole_rows = lax.all_gather(layer_input, "tensor", axis=1, tiled=True)
    normed = rms_scale(whole_rows, norm_gain)
    branch_x = jnp.dot(normed, in_weights[0], preferred_element_type=jnp.float32).astype(
        jnp.bfloat16
    )
    branch_y = jax.nn.gelu(
        jnp.dot(normed, in_weights[1], preferred_element_type=jnp.float32), approximate=True
    )
    num_tokens = branch_x.shape[0]
    rim_rows = conv_weight.shape[0] - 1
    earlier_rows = shifted(branch_x[num_tokens - rim_rows :], "seq", 1)
    padded = jnp.concatenate([earlier_rows, branch_x], axis=0).astype(jnp.float32)
    convolved = jnp.zeros(branch_x.shape, jnp.float32) + conv_bias
    for tap_index in range(conv_weight.shape[0]):
        start_row = rim_rows - tap_index
        convolved = convolved + conv_weight[tap_index] * padded[start_row : start_row + num_tokens]
    conv_out = convolved.astype(jnp.bfloat16)
    local_blocks = gate_weights.shape[1]
    block_width = gate_weights.shape[2]
    blocks_in = conv_out.reshape(num_tokens, local_blocks, block_width)
    gate_pre = jnp.einsum(
        "tnc,knce->ktne", blocks_in, gate_weights, preferred_element_type=jnp.float32
    )
    gate_pre = gate_pre.reshape(2, num_tokens, local_blocks * block_width) + gate_bias[:, None, :]
    log_decay = -8.0 * jax.nn.sigmoid(gate_pre[0]) * decay_rate
    decay = jnp.exp(log_decay)
    driven = (
        conv_out.astype(jnp.float32)
        * jax.nn.sigmoid(gate_pre[1])
        * jnp.sqrt(-jnp.expm1(2.0 * log_decay))
    )
    cum_decay, cum_state = lax.associative_scan(chain_step, (decay, driven), axis=0)
    identity = (jnp.ones_like(cum_decay[-1]), jnp.zeros_like(cum_state[-1]))
    entering = prefix((cum_decay[-1], cum_state[-1]), "seq", chain_step, identity)
    carried = entering[1]
    state = cum_decay * carried + cum_state
    mixed = (state * branch_y).astype(jnp.bfloat16)
    partial_sums = jnp.dot(mixed, out_weight, preferred_element_type=jnp.float32)
    full_sums = lax.psum(partial_sums.astype(jnp.bfloat16), "tensor").astype(jnp.float32)
    mid_full = (whole_rows.astype(jnp.float32) + full_sums).astype(jnp.bfloat16)
    own_width = layer_input.shape[1]
    residual = lax.dynamic_slice_in_dim(
        mid_full, lax.axis_index("tensor") * own_width, own_width, 1
    )
    mlp_normed = rms_scale(mid_full, mlp_gain)
    gate_up = jnp.einsum(
        "tr,krf->ktf",
        mlp_normed,
        lax.all_gather(mlp_in, "seq", axis=1, tiled=True),
        preferred_element_type=jnp.float32,
    )
    hidden = (jax.nn.gelu(gate_up[0], approximate=True) * gate_up[1]).astype(jnp.bfloat16)
    down_terms = jnp.dot(
        hidden,
        lax.all_gather(mlp_out, "seq", axis=1, tiled=True),
        preferred_element_type=jnp.float32,
    )
    down_share = lax.psum_scatter(
        down_terms.astype(jnp.bfloat16), "tensor", scatter_dimension=1, tiled=True
    ).astype(jnp.float32)
    return (residual.astype(jnp.float32) + down_share).astype(jnp.bfloat16)


def solution(mesh):
    return jax.shard_map(
        shards,
        mesh=mesh,
        in_specs=(
            P("seq", "tensor"),
            P(),
            P(None, None, "tensor"),
            P(None, "tensor"),
            P("tensor"),
            P(None, "tensor", None, None),
            P(None, "tensor"),
            P("tensor"),
            P("tensor", None),
            P(),
            P(None, "seq", "tensor"),
            P("tensor", "seq"),
        ),
        out_specs=P("seq", "tensor"),
        check_vma=False,
    )
```

profile of v0, /device:TPU:0, one launch (start us, length us, event | category | flops | bytes accessed | tf_op | source)
XLA Modules:
  0.0 835.9 jit_solution(12491428809460878877)
XLA Ops:
  7.4 0.7 all-gather.6.cloned.1.call-update
  8.1 0.9 fusion.115
  9.0 26.0 %all-gather.6.cloned.1.call-done = bf16[256,4096]{1,0:T(8,128)(2,1)} async-done(((bf16[256,1024]{1,0:T(8,128)(2,1)}), bf16[256,4096]{1,0:T(8,128)(2,1)}) %all-gather.6.cloned.1.call-update) | async-done | bytes 2097168 | tf_op jit(solution)/shard_map/all_gather | solution.py:54
  35.0 2.1 fusion.3
  37.2 4.1 fusion.26
  41.3 3.4 collective-permute-start
  44.7 1.3 collective-permute-done
  46.8 0.6 copy.18
  47.4 0.8 reshape.41
  48.4 0.8 fusion.91
  52.4 1.4 slice.328
  53.8 1.4 slice.367
  56.2 1.7 pad.129
  58.1 2.0 add_multiply_fusion.1
  60.2 1.7 pad.128
  61.8 0.7 add_bitcast_fusion
  62.5 27.9 %all-gather.1 = f32[8,1,512]{2,1,0:T(1,128)S(1)} all-gather(f32[1,1,512]{2,1,0:T(1,128)S(1)} %add_bitcast_fusion), channel_id=1, replica_groups=mesh['seq'=8,'tensor'=4] {'seq'}, dimensions={0}, use_global_device_ids=true | all-gather | bytes 18432 | tf_op jit(solution)/shard_map/all_gather | solution.py:15
  90.4 1.6 pad.113
  92.1 1.0 pad_maximum_fusion
  93.1 1.7 pad.112
  94.7 0.7 add_bitcast_fusion.1
  95.5 26.1 %all-gather = f32[8,1,512]{2,1,0:T(1,128)S(1)} all-gather(f32[1,1,512]{2,1,0:T(1,128)S(1)} %add_bitcast_fusion.1), channel_id=1, replica_groups=mesh['seq'=8,'tensor'=4] {'seq'}, dimensions={0}, use_global_device_ids=true | all-gather | bytes 18432 | tf_op jit(solution)/shard_map/all_gather | solution.py:15
  122.0 7.9 convolution_convert_fusion.1
  130.6 0.5 all-gather.10.cloned.1.call-update
  131.4 46.4 %all-reduce.34.cloned.1.call-done = bf16[256,4096]{1,0:T(8,128)(2,1)} async-done(((bf16[256,4096]{1,0:T(8,128)(2,1)}), bf16[256,4096]{1,0:T(8,128)(2,1)}) %all-reduce.34.cloned.1.call-update) | async-done | bytes 2097168 | tf_op jit(solution)/shard_map/psum | solution.py:92
  177.8 3.9 fusion
  181.7 427.0 %all-gather.8.cloned.1.call-done = bf16[2,4096,1536]{2,1,0:T(8,128)(2,1)} async-done(((bf16[2,512,1536]{2,1,0:T(8,128)(2,1)}), bf16[2,4096,1536]{2,1,0:T(8,128)(2,1)}) %all-gather.8.cloned.1.call-update) | async-done | bytes 25165840 | tf_op jit(solution)/shard_map/all_gather | solution.py:102
  608.7 13.4 %convolution_bitcast_fusion = f32[2,256,1536]{2,1,0:T(8,128)} fusion(bf16[2,4096,1536]{2,1,0:T(8,128)(2,1)} %all-gather.8.cloned.1.call-done, bf16[256,4096]{1,0:T(8,128)(2,1)} %get-tuple-element.129, f32[4096]{0:T(1024)S(1)} %copy-done.8, f32[256]{0:T(256)S(1)} %add_rsqrt_fusion), kind=kOutput, calls=%fused_computation.23 | convolution fusion | flops 6446645248 | bytes 30426112 | tf_op jit(solution)/shard_map/tr,krf->ktf/dot_general | solution.py:99
  622.1 164.4 %all-gather.10.cloned.1.call-done = bf16[1536,4096]{1,0:T(8,128)(2,1)} async-done(((bf16[1536,512]{1,0:T(8,128)(2,1)}), bf16[1536,4096]{1,0:T(8,128)(2,1)}) %all-gather.10.cloned.1.call-update) | async-done | bytes 12582928 | tf_op jit(solution)/shard_map/all_gather | solution.py:108
  786.5 10.6 %convolution_convert_fusion = bf16[256,4096]{1,0:T(8,128)(2,1)} fusion(bf16[1536,4096]{1,0:T(8,128)(2,1)} %all-gather.10.cloned.1.call-done, f32[2,256,1536]{2,1,0:T(8,128)} %convolution_bitcast_fusion), kind=kOutput, calls=%fused_computation.8 | convolution fusion | flops 3226206208 | bytes 17825792 | tf_op jit(solution)/shard_map/dot_general | solution.py:106
  797.1 29.5 %reduce-scatter.2.cloned.1.call-done = bf16[256,1024]{1,0:T(8,128)(2,1)} async-done(((bf16[256,4096]{1,0:T(8,128)(2,1)}), bf16[256,1024]{1,0:T(8,128)(2,1)}) %reduce-scatter.2.cloned.1.call-update) | async-done | bytes 524304 | tf_op jit(solution)/shard_map/reduce_scatter | solution.py:111
  826.6 2.2 add_convert_fusion
  (168 shorter events, 6.3 us)
Async XLA Ops:
  7.4 39.1 %copy-start = (bf16[2,2,256,256]{3,2,1,0:T(8,128)(2,1)S(1)}, bf16[2,2,256,256]{3,2,1,0:T(8,128)(2,1)}, u32[]{:S(2)}) copy-start(bf16[2,2,256,256]{3,2,1,0:T(8,128)(2,1)} %param.19) | copy-start | bytes 1572868
  7.4 27.7 %all-gather.6.cloned.1.call-start = ((), (), s32[]{:S(2)}) async-start(), calls=%async_computation.1 | async-start | bytes 2621440 | tf_op jit(solution)/shard_map/all_gather | solution.py:54
  8.1 169.7 %all-reduce.34.cloned.1.call-start = ((), (), s32[]{:S(2)}) async-start(), calls=%async_computation.2 | async-start | bytes 4194304 | tf_op jit(solution)/shard_map/psum | solution.py:92
  37.1 7.6 copy-start.6
  37.1 9.0 %copy-start.4 = (f32[512]{0:T(512)S(1)}, f32[512]{0:T(512)}, u32[]{:S(2)}) copy-start(f32[512]{0:T(512)} %param.18) | copy-start | bytes 6148
  41.3 4.7 collective-permute-start
  46.4 1.8 copy-start.5
  58.1 63.9 %copy-start.2 = (bf16[256,4096]{1,0:T(8,128)(2,1)S(1)}, bf16[256,4096]{1,0:T(8,128)(2,1)}, u32[]{:S(2)}) copy-start(bf16[256,4096]{1,0:T(8,128)(2,1)} %all-gather.6.cloned.1.call-done) | copy-start | bytes 6291460
  58.1 63.9 %copy-start.7 = (f32[4096]{0:T(1024)S(1)}, f32[4096]{0:T(1024)}, u32[]{:S(2)}) copy-start(f32[4096]{0:T(1024)} %param.15) | copy-start | bytes 49156
  60.1 61.9 %copy-start.3 = (f32[256,512]{1,0:T(8,128)S(1)}, f32[256,512]{1,0:T(8,128)}, u32[]{:S(2)}) copy-start(f32[256,512]{1,0:T(8,128)} %pad.129) | copy-start | bytes 1572868
  130.0 478.7 %all-gather.8.cloned.1.call-start = ((), (), s32[]{:S(2)}) async-start(), calls=%async_computation.3 | async-start | bytes 28311552 | tf_op jit(solution)/shard_map/all_gather | solution.py:102
  130.6 656.0 %all-gather.10.cloned.1.call-start = ((), (), s32[]{:S(2)}) async-start(), calls=%async_computation.4 | async-start | bytes 14155776 | tf_op jit(solution)/shard_map/all_gather | solution.py:108
  131.2 477.6 %copy-start.8 = (f32[4096]{0:T(1024)S(1)}, f32[4096]{0:T(1024)}, u32[]{:S(2)}) copy-start(f32[4096]{0:T(1024)} %param.23) | copy-start | bytes 49156
  131.2 695.4 %reduce-scatter.2.cloned.1.call-start = ((), (), s32[]{:S(2)}) async-start(), calls=%async_computation.5 | async-start | bytes 2621440 | tf_op jit(solution)/shard_map/reduce_scatter | solution.py:111
  786.5 42.3 %copy-start.1 = (bf16[2,2,256,256]{3,2,1,0:T(8,128)(2,1)S(1)}, bf16[2,2,256,256]{3,2,1,0:T(8,128)(2,1)}, u32[]{:S(2)}) copy-start(bf16[2,2,256,256]{3,2,1,0:T(8,128)(2,1)} %param.19) | copy-start | bytes 1572868
Sparse Core Ops, SparseCore 0:
  9.7 25.2 all-gather.5
  130.1 47.6 all-reduce.33
  797.2 29.3 reduce-scatter.1
Sparse Core Ops, SparseCore 1:
  132.0 476.6 all-gather.7
  610.6 175.9 all-gather.9
where the time goes:
time: 836 us
  waiting for transfers between devices  696 us (83%)
  blocking collectives  54 us (6%)
  matrix products  36.4 us (4%)
  between operations  15.4 us (2%)
  local copies, waits for them, and re-layouts  15.1 us (2%)
  other arithmetic  14.7 us (2%)
    all_gather x1, waiting for transfers between devices, shards(): lax.all_gather(mlp_in, 'seq', axis=1, tiled=True)  427 us
    all_gather x1, waiting for transfers between devices, shards(): lax.all_gather(mlp_out, 'seq', axis=1, tiled=True)  164 us
    all_gather x2, blocking collectives, prefix(): everything = jax.tree.map(lambda part: lax.all_gather(part, axis), value)  54 us
    psum x1, waiting for transfers between devices, shards(): lax.psum(partial_sums.astype(jnp.bfloat16), 'tensor').astype(jnp.float32)  46.4 us
    reduce_scatter x1, waiting for transfers between devices, shards(): lax.psum_scatter(down_terms.astype(jnp.bfloat16), 'tensor', scatter_dimen...  29.5 us
    all_gather x1, waiting for transfers between devices, shards(): whole_rows = lax.all_gather(layer_input, 'tensor', axis=1, tiled=True)  26 us
  transfers between devices with their start and end apart: 6, of which 6 were waited for; matrix products, arithmetic and copies ran while one was open for 2% of the time, Pallas kernels for 0%

commit v1 on v0

--- a/solution.py
+++ b/solution.py
@@ -2,6 +2,22 @@
 import jax.numpy as jnp
 from jax import lax
 from jax.sharding import PartitionSpec as P
+
+
+def ring_product(value, axis, dim, term):
+    count, index, rows = (lax.axis_size(axis), lax.axis_index(axis), value.shape[dim])
+    forward = [(i, (i + 1) % count) for i in range(count)]
+    left = [(i, (i - 1) % count) for i in range(count)]
+    half = count // 2
+    from_left = from_right = value
+    subtotal = term(value, index * rows)
+    for step in range(1, half + 1):
+        from_left = lax.ppermute(from_left, axis, forward)
+        if step < count - half:
+            from_right = lax.ppermute(from_right, axis, left)
+            subtotal = subtotal + term(from_right, (index + step) % count * rows)
+        subtotal = subtotal + term(from_left, (index - step) % count * rows)
+    return subtotal
 
 
 def shifted(value, axis, steps):
@@ -96,11 +112,16 @@
         mid_full, lax.axis_index("tensor") * own_width, own_width, 1
     )
     mlp_normed = rms_scale(mid_full, mlp_gain)
-    gate_up = jnp.einsum(
-        "tr,krf->ktf",
-        mlp_normed,
-        lax.all_gather(mlp_in, "seq", axis=1, tiled=True),
-        preferred_element_type=jnp.float32,
+    gate_up = ring_product(
+        mlp_in,
+        "seq",
+        1,
+        lambda part_2, start_2: jnp.einsum(
+            "tr,krf->ktf",
+            lax.dynamic_slice_in_dim(mlp_normed, start_2, part_2.shape[1], axis=1),
+            part_2,
+            preferred_element_type=jnp.float32,
+        ),
     )
     hidden = (jax.nn.gelu(gate_up[0], approximate=True) * gate_up[1]).astype(jnp.bfloat16)
     down_terms = jnp.dot(

time: 836 us -> 735 us (0.88)
  waiting for transfers between devices: 696 us -> 573 us
  starting transfers between devices: 3.72 us -> 19.9 us
    ppermute x0 -> x7, waiting for transfers between devices: none -> 517 us  [the longest x4 461 us: ring_product(): from_left = lax.ppermute(from_left, axis, forward)]
    all_gather x1 -> x0, waiting for transfers between devices: 427 us -> none  [shards(): lax.all_gather(mlp_in, 'seq', axis=1, tiled=True)]
    all_gather x1, waiting for transfers between devices: 164 us -> 0.01 us  [shards(): lax.all_gather(mlp_out, 'seq', axis=1, tiled=True)]
    psum x1, waiting for transfers between devices: 46.4 us -> 0.01 us  [shards(): lax.psum(partial_sums.astype(jnp.bfloat16), 'tensor').astype(jnp.float32)]
    ppermute x0 -> x7, starting transfers between devices: none -> 16.4 us  [the longest x3 8.92 us: ring_product(): from_right = lax.ppermute(from_right, axis, left)]
    dot_general x1 -> x8, matrix products: 13.4 us -> 17.5 us  [shards(): jnp.einsum('tr,krf->ktf', lax.dynamic_slice_in_dim(mlp_normed, start_2, p...]
  transfers between devices with their start and end apart: 6 -> 12, of which waited for: 6 -> 8; matrix products, arithmetic and copies ran while one was open for 2% -> 3% of each run, Pallas kernels for 0% -> 0%
where the time goes in v1:
time: 735 us
  waiting for transfers between devices  573 us (78%)
  blocking collectives  54 us (7%)
  matrix products  40.5 us (6%)
  starting transfers between devices  19.9 us (3%)
  local copies, waits for them, and re-layouts  16.9 us (2%)
  between operations  15.5 us (2%)
  other arithmetic  14.6 us (2%)
    ppermute x4, waiting for transfers between devices, ring_product(): from_left = lax.ppermute(from_left, axis, forward)  461 us
    ppermute x3, waiting for transfers between devices, ring_product(): from_right = lax.ppermute(from_right, axis, left)  55.8 us
    all_gather x2, blocking collectives, prefix(): everything = jax.tree.map(lambda part: lax.all_gather(part, axis), value)  54 us
    reduce_scatter x1, waiting for transfers between devices, shards(): lax.psum_scatter(down_terms.astype(jnp.bfloat16), 'tensor', scatter_dimen...  27.6 us
    all_gather x1, waiting for transfers between devices, shards(): whole_rows = lax.all_gather(layer_input, 'tensor', axis=1, tiled=True)  26 us
    dot_general x8, matrix products, shards(): jnp.einsum('tr,krf->ktf', lax.dynamic_slice_in_dim(mlp_normed, start_2, p...  17.5 us
  transfers between devices with their start and end apart: 12, of which 8 were waited for; matrix products, arithmetic and copies ran while one was open for 3% of the time, Pallas kernels for 0%

profile of v1, /device:TPU:0, one launch (start us, length us, event | category | flops | bytes accessed | tf_op | source)
XLA Modules:
  0.0 734.6 jit_solution(9497658108886503266)
XLA Ops:
  9.0 26.0 %all-gather.5.cloned.1.call-done = bf16[256,4096]{1,0:T(8,128)(2,1)} async-done(((bf16[256,1024]{1,0:T(8,128)(2,1)}), bf16[256,4096]{1,0:T(8,128)(2,1)}) %all-gather.5.cloned.1.call-update) | async-done | bytes 2097168 | tf_op jit(solution)/shard_map/all_gather | solution.py:70
  35.0 2.1 fusion.3
  37.2 4.1 fusion.25
  41.3 3.4 collective-permute-start
  56.3 1.6 pad.129
  58.1 2.0 add_multiply_fusion.1
  60.1 1.7 pad.128
  62.5 27.9 %all-gather.1 = f32[8,1,512]{2,1,0:T(1,128)S(1)} all-gather(f32[1,1,512]{2,1,0:T(1,128)S(1)} %add_bitcast_fusion), channel_id=1, replica_groups=mesh['seq'=8,'tensor'=4] {'seq'}, dimensions={0}, use_global_device_ids=true | all-gather | bytes 18432 | tf_op jit(solution)/shard_map/all_gather | solution.py:31
  90.4 1.7 pad.113
  93.1 1.7 pad.112
  95.6 26.1 %all-gather = f32[8,1,512]{2,1,0:T(1,128)S(1)} all-gather(f32[1,1,512]{2,1,0:T(1,128)S(1)} %add_bitcast_fusion.1), channel_id=1, replica_groups=mesh['seq'=8,'tensor'=4] {'seq'}, dimensions={0}, use_global_device_ids=true | all-gather | bytes 18432 | tf_op jit(solution)/shard_map/all_gather | solution.py:31
  122.1 7.9 %convolution_convert_fusion.1 = bf16[256,4096]{1,0:T(8,128)(2,1)} fusion(bf16[512,4096]{1,0:T(8,128)(2,1)} %param.22, bf16[2,4096,512]{2,1,0:T(8,128)(2,1)} %param.16, bf16[256,4096]{1,0:T(8,128)(2,1)S(1)} %copy-done.2, f32[4096]{0:T(1024)S(1)} %copy-done.11, f32[256]{0:T(256)S(1)} %add_rsqrt_fusion.1, f32[256,512]{1,0:T(8,128)} %pad.128, ...), kind=kOutput, calls=%fused_computation.9 | convolution fusion | flops 2154561536 | bytes 14699520 | tf_op jit(solution)/shard_map/dot_general | solution.py:107
  130.8 4.7 collective-permute-start.1
  135.5 143.4 %collective-permute-done.2 = bf16[2,512,1536]{2,1,0:T(8,128)(2,1)S(1)} collective-permute-done((bf16[2,512,1536]{2,1,0:T(8,128)(2,1)}, bf16[2,512,1536]{2,1,0:T(8,128)(2,1)S(1)}, u32[]{:S(2)}, u32[]{:S(2)}) %collective-permute-start.2) | collective-permute-done | bytes 3145760 | tf_op jit(solution)/shard_map/ppermute | solution.py:15
  278.9 1.7 copy-done.3
  280.6 2.4 collective-permute-start.4
  283.3 2.0 collective-permute-start.3
  285.3 189.8 %collective-permute-done.4 = bf16[2,512,1536]{2,1,0:T(8,128)(2,1)} collective-permute-done((bf16[2,512,1536]{2,1,0:T(8,128)(2,1)S(1)}, bf16[2,512,1536]{2,1,0:T(8,128)(2,1)}, u32[]{:S(2)}, u32[]{:S(2)}) %collective-permute-start.4) | collective-permute-done | bytes 3145760 | tf_op jit(solution)/shard_map/ppermute | solution.py:15
  475.1 2.6 collective-permute-start.6
  477.7 3.2 fusion
  481.0 2.2 collective-permute-start.5
  484.0 127.7 %collective-permute-done.6 = bf16[2,512,1536]{2,1,0:T(8,128)(2,1)} collective-permute-done((bf16[2,512,1536]{2,1,0:T(8,128)(2,1)}, bf16[2,512,1536]{2,1,0:T(8,128)(2,1)}, u32[]{:S(2)}, u32[]{:S(2)}) %collective-permute-start.6) | collective-permute-done | bytes 3145760 | tf_op jit(solution)/shard_map/ppermute | solution.py:15
  611.7 2.5 collective-permute-start.7
  615.2 3.0 convolution_add_fusion.4
  619.3 2.9 fusion.86
  622.2 3.0 fusion.14
  625.2 2.9 fusion.83
  628.1 55.4 %collective-permute-done.5 = bf16[2,512,1536]{2,1,0:T(8,128)(2,1)S(1)} collective-permute-done((bf16[2,512,1536]{2,1,0:T(8,128)(2,1)}, bf16[2,512,1536]{2,1,0:T(8,128)(2,1)S(1)}, u32[]{:S(2)}, u32[]{:S(2)}) %collective-permute-start.5) | collective-permute-done | bytes 3145760 | tf_op jit(solution)/shard_map/ppermute | solution.py:17
  684.5 2.6 fusion.15
  687.2 10.6 %convolution_convert_fusion = bf16[256,4096]{1,0:T(8,128)(2,1)} fusion(bf16[1536,4096]{1,0:T(8,128)(2,1)} %all-gather.7.cloned.1.call-done, f32[2,256,1536]{2,1,0:T(8,128)} %fusion.15), kind=kOutput, calls=%fused_computation.8 | convolution fusion | flops 3226206208 | bytes 17825792 | tf_op jit(solution)/shard_map/dot_general | solution.py:127
  697.8 27.6 %reduce-scatter.2.cloned.1.call-done = bf16[256,1024]{1,0:T(8,128)(2,1)} async-done(((bf16[256,4096]{1,0:T(8,128)(2,1)}), bf16[256,1024]{1,0:T(8,128)(2,1)}) %reduce-scatter.2.cloned.1.call-update) | async-done | bytes 524304 | tf_op jit(solution)/shard_map/reduce_scatter | solution.py:132
  725.4 2.0 add_convert_fusion
  (193 shorter events, 20.6 us)
Async XLA Ops:
  7.4 39.1 %copy-start = (bf16[2,2,256,256]{3,2,1,0:T(8,128)(2,1)S(1)}, bf16[2,2,256,256]{3,2,1,0:T(8,128)(2,1)}, u32[]{:S(2)}) copy-start(bf16[2,2,256,256]{3,2,1,0:T(8,128)(2,1)} %param.19) | copy-start | bytes 1572868
  7.4 27.7 %all-gather.5.cloned.1.call-start = ((), (), s32[]{:S(2)}) async-start(), calls=%async_computation.1 | async-start | bytes 2621440 | tf_op jit(solution)/shard_map/all_gather | solution.py:70
  8.1 469.6 %all-reduce.34.cloned.1.call-start = ((), (), s32[]{:S(2)}) async-start(), calls=%async_computation.2 | async-start | bytes 4194304 | tf_op jit(solution)/shard_map/psum | solution.py:108
  37.1 7.6 %copy-start.10 = (f32[512]{0:T(512)S(1)}, f32[512]{0:T(512)}, u32[]{:S(2)}) copy-start(f32[512]{0:T(512)} %param.21) | copy-start | bytes 6148
  37.1 9.0 %copy-start.8 = (f32[512]{0:T(512)S(1)}, f32[512]{0:T(512)}, u32[]{:S(2)}) copy-start(f32[512]{0:T(512)} %param.18) | copy-start | bytes 6148
  41.3 4.7 collective-permute-start
  46.4 1.8 copy-start.9
  58.0 64.1 %copy-start.2 = (bf16[256,4096]{1,0:T(8,128)(2,1)S(1)}, bf16[256,4096]{1,0:T(8,128)(2,1)}, u32[]{:S(2)}) copy-start(bf16[256,4096]{1,0:T(8,128)(2,1)} %all-gather.5.cloned.1.call-done) | copy-start | bytes 6291460
  58.1 64.1 %copy-start.11 = (f32[4096]{0:T(1024)S(1)}, f32[4096]{0:T(1024)}, u32[]{:S(2)}) copy-start(f32[4096]{0:T(1024)} %param.15) | copy-start | bytes 49156
  60.1 62.0 %copy-start.6 = (f32[256,512]{1,0:T(8,128)S(1)}, f32[256,512]{1,0:T(8,128)}, u32[]{:S(2)}) copy-start(f32[256,512]{1,0:T(8,128)} %pad.129) | copy-start | bytes 1572868
  130.1 557.1 %all-gather.7.cloned.1.call-start = ((), (), s32[]{:S(2)}) async-start(), calls=%async_computation.3 | async-start | bytes 14155776 | tf_op jit(solution)/shard_map/all_gather | solution.py:129
  130.6 594.8 %reduce-scatter.2.cloned.1.call-start = ((), (), s32[]{:S(2)}) async-start(), calls=%async_computation.4 | async-start | bytes 2621440 | tf_op jit(solution)/shard_map/reduce_scatter | solution.py:132
  130.7 148.2 %collective-permute-start.2 = (bf16[2,512,1536]{2,1,0:T(8,128)(2,1)}, bf16[2,512,1536]{2,1,0:T(8,128)(2,1)S(1)}, u32[]{:S(2)}, u32[]{:S(2)}) collective-permute-start(bf16[2,512,1536]{2,1,0:T(8,128)(2,1)} %param.24), channel_id=1, source_target_pairs={{0,4},{4,8},{8,12},{12,16},{16,20},{20,24},{24,28},{28,0},{1,5},{5... | collective-permute-start | bytes 9437192 | tf_op jit(solution)/shard_map/ppermute | solution.py:15
  130.8 152.6 %collective-permute-start.1 = (bf16[2,512,1536]{2,1,0:T(8,128)(2,1)}, bf16[2,512,1536]{2,1,0:T(8,128)(2,1)}, u32[]{:S(2)}, u32[]{:S(2)}) collective-permute-start(bf16[2,512,1536]{2,1,0:T(8,128)(2,1)} %param.24), channel_id=1, source_target_pairs={{0,28},{4,0},{8,4},{12,8},{16,12},{20,16},{24,20},{28,24},{1,29},{... | collective-permute-start | bytes 9437192 | tf_op jit(solution)/shard_map/ppermute | solution.py:17
  278.9 1.7 copy-start.3
  280.6 194.5 %collective-permute-start.4 = (bf16[2,512,1536]{2,1,0:T(8,128)(2,1)S(1)}, bf16[2,512,1536]{2,1,0:T(8,128)(2,1)}, u32[]{:S(2)}, u32[]{:S(2)}) collective-permute-start(bf16[2,512,1536]{2,1,0:T(8,128)(2,1)S(1)} %collective-permute-done.2), channel_id=1, source_target_pairs={{0,4},{4,8},{8,12},{12,16},{16,20},{20,24},{24,28},{28,0},{1,5},{5... | collective-permute-start | bytes 9437192 | tf_op jit(solution)/shard_map/ppermute | solution.py:15
  283.3 197.7 %collective-permute-start.3 = (bf16[2,512,1536]{2,1,0:T(8,128)(2,1)}, bf16[2,512,1536]{2,1,0:T(8,128)(2,1)}, u32[]{:S(2)}, u32[]{:S(2)}) collective-permute-start(bf16[2,512,1536]{2,1,0:T(8,128)(2,1)} %collective-permute-done.1), channel_id=1, source_target_pairs={{0,28},{4,0},{8,4},{12,8},{16,12},{20,16},{24,20},{28,24},{1,29},{... | collective-permute-start | bytes 9437192 | tf_op jit(solution)/shard_map/ppermute | solution.py:17
  475.1 136.5 %collective-permute-start.6 = (bf16[2,512,1536]{2,1,0:T(8,128)(2,1)}, bf16[2,512,1536]{2,1,0:T(8,128)(2,1)}, u32[]{:S(2)}, u32[]{:S(2)}) collective-permute-start(bf16[2,512,1536]{2,1,0:T(8,128)(2,1)} %collective-permute-done.4), channel_id=1, source_target_pairs={{0,4},{4,8},{8,12},{12,16},{16,20},{20,24},{24,28},{28,0},{1,5},{5... | collective-permute-start | bytes 9437192 | tf_op jit(solution)/shard_map/ppermute | solution.py:15
  477.7 5.5 copy-start.7
  481.0 133.2 %copy-start.5 = (bf16[2,512,1536]{2,1,0:T(8,128)(2,1)S(1)}, bf16[2,512,1536]{2,1,0:T(8,128)(2,1)}, u32[]{:S(2)}) copy-start(bf16[2,512,1536]{2,1,0:T(8,128)(2,1)} %param.24) | copy-start | bytes 9437188
  481.0 202.5 %collective-permute-start.5 = (bf16[2,512,1536]{2,1,0:T(8,128)(2,1)}, bf16[2,512,1536]{2,1,0:T(8,128)(2,1)S(1)}, u32[]{:S(2)}, u32[]{:S(2)}) collective-permute-start(bf16[2,512,1536]{2,1,0:T(8,128)(2,1)} %collective-permute-done.3), channel_id=1, source_target_pairs={{0,28},{4,0},{8,4},{12,8},{16,12},{20,16},{24,20},{28,24},{1,29},{... | collective-permute-start | bytes 9437192 | tf_op jit(solution)/shard_map/ppermute | solution.py:17
  611.7 72.8 %collective-permute-start.7 = (bf16[2,512,1536]{2,1,0:T(8,128)(2,1)}, bf16[2,512,1536]{2,1,0:T(8,128)(2,1)S(1)}, u32[]{:S(2)}, u32[]{:S(2)}) collective-permute-start(bf16[2,512,1536]{2,1,0:T(8,128)(2,1)} %collective-permute-done.6), channel_id=1, source_target_pairs={{0,4},{4,8},{8,12},{12,16},{16,20},{20,24},{24,28},{28,0},{1,5},{5... | collective-permute-start | bytes 9437192 | tf_op jit(solution)/shard_map/ppermute | solution.py:15
  615.1 3.1 copy-start.4
  687.2 40.3 %copy-start.1 = (bf16[2,2,256,256]{3,2,1,0:T(8,128)(2,1)S(1)}, bf16[2,2,256,256]{3,2,1,0:T(8,128)(2,1)}, u32[]{:S(2)}) copy-start(bf16[2,2,256,256]{3,2,1,0:T(8,128)(2,1)} %param.19) | copy-start | bytes 1572868
Sparse Core Ops, SparseCore 0:
  9.7 25.2 all-gather.4
  130.2 47.6 all-reduce.33
  697.9 27.4 reduce-scatter.1
Sparse Core Ops, SparseCore 1:
  132.6 393.9 all-gather.6
